TPU v7x, 32 devices: a whole 2x2x4 slice. The times are simulated.
32 devices in a mesh: wide: 16 (over z, y, core), narrow: 2 (over x).
Axes of the slice: x: 2, y: 2, z: 4, core: 2. Of those that a mesh axis runs over, the one named last changes fastest.
Arguments:
- hidden_in: bfloat16 [16384, 1024], P(('wide', 'narrow')), may hold values from -6 to 6
- segment_ids: int32 [32, 512], P(('wide', 'narrow')), may hold values from 0 to 7, never falling along the last dimension, each value on 1 to 256 neighbouring positions
- expert_ids: int32 [16384, 8], P(('wide', 'narrow')), may hold values from 0 to 15, all different within a row; in each aligned block of 512 rows (0 to 511, 512 to 1023, ...) at most 512 rows name the same one
- attn_gain: float32 [1024], replicated, may hold values from 0.5 to 1.5
- w_query: bfloat16 [1024, 1024], replicated, may hold values from -0.1875 to 0.1875
- w_key: bfloat16 [1024, 512], replicated, may hold values from -0.1875 to 0.1875
- w_value: bfloat16 [1024, 512], replicated, may hold values from -0.1875 to 0.1875
- w_out: bfloat16 [1024, 1024], replicated, may hold values from -0.75 to 0.75
- ffn_gain: float32 [1024], replicated, may hold values from 0.5 to 1.5
- router: bfloat16 [1024, 16], replicated, may hold values from -0.1875 to 0.1875
- w_gate: bfloat16 [16, 1024, 512], P('wide', None, 'narrow'), may hold values from -0.1875 to 0.1875
- w_up: bfloat16 [16, 1024, 512], P('wide', None, 'narrow'), may hold values from -0.1875 to 0.1875
- w_down: bfloat16 [16, 512, 1024], P('wide', 'narrow'), may hold values from -0.75 to 0.75
- grad_out: bfloat16 [16384, 1024], P(('wide', 'narrow')), may hold values from -6 to 6
Outputs:
- hidden_out: bfloat16 [16384, 1024], P(('wide', 'narrow'))
- grad_in: bfloat16 [16384, 1024], P(('wide', 'narrow'))
- grad_attn_gain: float32 [1024], replicated
- grad_query: float32 [1024, 1024], replicated
- grad_key: float32 [1024, 512], replicated
- grad_value: float32 [1024, 512], replicated
- grad_out_proj: float32 [1024, 1024], replicated
- grad_ffn_gain: float32 [1024], replicated
- grad_router: float32 [1024, 16], replicated
- grad_gate: float32 [16, 1024, 512], P('wide', None, 'narrow')
- grad_up: float32 [16, 1024, 512], P('wide', None, 'narrow')
- grad_down: float32 [16, 512, 1024], P('wide', 'narrow')
Inputs may be any that keep to these rules, and one draw needn't show every extreme that they name: `segment_ids`: each packed row has 8 documents numbered in order from 0, each of 1 to half of 512 tokens, one of exactly half of 512. `expert_ids`: each token names 8 different experts. Among the 512 tokens of one packed row no expert is named more than 512 times, and in every draw some row names some expert exactly 512 times.
All inputs are finite; a program needn't handle non-finite values.
Results may differ from a plain program's by a relative error of at most 0.015.
Values may be sent and summed in bfloat16 or wider, within the bound.
A program may use at most 320 MiB of HBM per device.

v0:
```python
import jax
import jax.numpy as jnp
from jax import lax
from jax.sharding import PartitionSpec as P

HD = 64
EPSILON = 1e-05


def norm_scale(values):
    return lax.rsqrt(jnp.mean(values * values, axis=-1, keepdims=True) + EPSILON)


def norm_back(values, inv_rms, gain_vector, grad_rows):
    weighted = grad_rows * gain_vector
    inner = jnp.mean(weighted * values, axis=-1, keepdims=True)
    value_grad = inv_rms * weighted - values * (inv_rms * inv_rms * inv_rms) * inner
    return (value_grad, jnp.sum(grad_rows * values * inv_rms, axis=0))


def rope_tables(length, head_dim):
    half_size = head_dim // 2
    freqs = 10000.0 ** (-(jnp.arange(half_size, dtype=jnp.float32) * 2.0) / head_dim)
    angles = jnp.arange(length, dtype=jnp.float32)[:, None] * freqs[None, :]
    return (jnp.cos(angles), jnp.sin(angles))


def rotate(values, cosine_table, sine_table, direction):
    half_size = values.shape[-1] // 2
    first_half = values[..., :half_size]
    second_half = values[..., half_size:]
    cosine_part = cosine_table[:, None, :]
    sine_part = sine_table[:, None, :] * direction
    return jnp.concatenate(
        [
            first_half * cosine_part - second_half * sine_part,
            second_half * cosine_part + first_half * sine_part,
        ],
        axis=-1,
    )


def attention_probs(grouped, key_rows, allowed, head_dim):
    scores = jnp.einsum(
        "qngd,knd->ngqk", grouped, key_rows, preferred_element_type=jnp.float32
    ) * head_dim ** (-0.5)
    return jnp.where(allowed, scores, -1e30)


def on_device(
    hidden_in,
    segment_ids,
    expert_ids,
    attn_gain,
    w_query,
    w_key,
    w_value,
    w_out,
    ffn_gain,
    router,
    w_gate,
    w_up,
    w_down,
    grad_out,
):
    f32 = jnp.float32
    bf16 = jnp.bfloat16
    length, model_width = hidden_in.shape
    head_dim = HD
    head_count = w_query.shape[1] // head_dim
    kv_count = w_key.shape[1] // head_dim
    group_size = head_count // kv_count
    experts = router.shape[1]
    rows_grad = lax.all_gather(grad_out, "wide", axis=0, tiled=True)
    full_gate, full_up, full_down = (
        lax.all_gather(w_gate, "narrow", axis=2, tiled=True),
        lax.all_gather(w_up, "narrow", axis=2, tiled=True),
        lax.all_gather(w_down, "narrow", axis=1, tiled=True),
    )
    inputs = hidden_in.astype(f32)
    scale_one = norm_scale(inputs)
    normed = (inputs * scale_one * attn_gain).astype(bf16)
    query_pre = jnp.dot(normed, w_query, preferred_element_type=f32)
    key_pre = jnp.dot(normed, w_key, preferred_element_type=f32)
    value_pre = jnp.dot(normed, w_value, preferred_element_type=f32)
    cosine_table, sine_table = rope_tables(length, head_dim)
    query_rows = rotate(
        query_pre.reshape(length, head_count, head_dim), cosine_table, sine_table, 1.0
    ).astype(bf16)
    key_rows = rotate(
        key_pre.reshape(length, kv_count, head_dim), cosine_table, sine_table, 1.0
    ).astype(bf16)
    value_rows = value_pre.astype(bf16).reshape(length, kv_count, head_dim)
    grouped = query_rows.reshape(length, kv_count, group_size, head_dim)
    segments = segment_ids[0]
    places = jnp.arange(length, dtype=jnp.int32)
    allowed = (segments[:, None] == segments[None, :]) & (places[:, None] >= places[None, :])
    scores = attention_probs(grouped, key_rows, allowed, head_dim)
    row_max = jnp.max(scores, axis=-1, keepdims=True)
    log_total = row_max + jnp.log(jnp.sum(jnp.exp(scores - row_max), axis=-1, keepdims=True))
    weights_prob = jnp.exp(scores - log_total)
    attended = jnp.einsum(
        "ngqk,knd->qngd", weights_prob.astype(bf16), value_rows, preferred_element_type=f32
    )
    attended = attended.reshape(length, head_count * head_dim).astype(bf16)
    mixed_rows = inputs + jnp.dot(attended, w_out, preferred_element_type=f32)
    scale_two = norm_scale(mixed_rows)
    ffn_normed = (mixed_rows * scale_two * ffn_gain).astype(bf16)
    logits = jnp.dot(ffn_normed, router, preferred_element_type=f32)
    picked = expert_ids[:, :, None] == jnp.arange(experts, dtype=jnp.int32)[None, None, :]
    member = jnp.any(picked, axis=1)
    masked = jnp.where(member, logits, -jnp.inf)
    powers = jnp.where(member, jnp.exp(masked - jnp.max(masked, axis=-1, keepdims=True)), 0.0)
    gate_probs = powers / jnp.sum(powers, axis=-1, keepdims=True)
    row_gates = lax.all_to_all(gate_probs.T, "wide", split_axis=0, concat_axis=0, tiled=True)
    row_gates = row_gates.reshape(-1, 1)
    rows_in = lax.all_gather(ffn_normed, "wide", axis=0, tiled=True)
    gate_act = jnp.dot(rows_in, full_gate[0], preferred_element_type=f32)
    up_act = jnp.dot(rows_in, full_up[0], preferred_element_type=f32)
    hidden_act = (jax.nn.silu(gate_act) * up_act).astype(bf16)
    outputs = jnp.dot(hidden_act, full_down[0], preferred_element_type=f32).astype(bf16)
    moe_rows = lax.psum_scatter(
        (row_gates * outputs.astype(f32)).astype(bf16), "wide", scatter_dimension=0, tiled=True
    )
    hidden_out = (mixed_rows + moe_rows.astype(f32)).astype(bf16)
    cotangent = grad_out.astype(f32)
    gate_dots = jnp.sum(outputs.astype(f32) * rows_grad.astype(f32), axis=-1)
    gate_grads = lax.all_to_all(
        gate_dots.reshape(experts, length), "wide", split_axis=0, concat_axis=0, tiled=True
    ).T
    logit_grads = (
        gate_probs * (gate_grads - jnp.sum(gate_probs * gate_grads, axis=-1, keepdims=True))
    ).astype(bf16)
    router_grad = jnp.einsum("sd,se->de", ffn_normed, logit_grads, preferred_element_type=f32)
    normed_two_grad = jnp.einsum("se,de->sd", logit_grads, router, preferred_element_type=f32)
    grads_in = (row_gates * rows_grad.astype(f32)).astype(bf16)
    hidden_grad = jnp.einsum("rd,fd->rf", grads_in, full_down[0], preferred_element_type=f32)
    down_w_grad = jnp.einsum("rf,rd->fd", hidden_act, grads_in, preferred_element_type=f32)
    sigmoid_gate = jax.nn.sigmoid(gate_act)
    gate_grad = (
        hidden_grad * up_act * sigmoid_gate * (1.0 + gate_act * (1.0 - sigmoid_gate))
    ).astype(bf16)
    up_grad = (hidden_grad * gate_act * sigmoid_gate).astype(bf16)
    gate_w_grad = jnp.einsum("rd,rf->df", rows_in, gate_grad, preferred_element_type=f32)
    up_w_grad = jnp.einsum("rd,rf->df", rows_in, up_grad, preferred_element_type=f32)
    copy_grads = (
        jnp.einsum("rf,df->rd", gate_grad, full_gate[0], preferred_element_type=f32)
        + jnp.einsum("rf,df->rd", up_grad, full_up[0], preferred_element_type=f32)
    ).astype(bf16)
    rows_back = lax.psum_scatter(copy_grads, "wide", scatter_dimension=0, tiled=True)
    gate_w_grad, up_w_grad, down_w_grad = (
        lax.psum_scatter(
            gate_w_grad[None].astype(jnp.bfloat16), "narrow", scatter_dimension=2, tiled=True
        ).astype(jnp.float32),
        lax.psum_scatter(
            up_w_grad[None].astype(jnp.bfloat16), "narrow", scatter_dimension=2, tiled=True
        ).astype(jnp.float32),
        lax.psum_scatter(
            down_w_grad[None].astype(jnp.bfloat16), "narrow", scatter_dimension=1, tiled=True
        ).astype(jnp.float32),
    )
    normed_two_grad = normed_two_grad + rows_back.astype(f32)
    mixed_part, ffn_gain_grad = norm_back(mixed_rows, scale_two, ffn_gain, normed_two_grad)
    mixed_grad = cotangent + mixed_part
    branch_grad = mixed_grad.astype(bf16)
    out_w_grad = jnp.einsum("sh,sd->hd", attended, branch_grad, preferred_element_type=f32)
    attended_grad = jnp.einsum("sd,hd->sh", branch_grad, w_out, preferred_element_type=f32).astype(
        bf16
    )
    attended_grad = attended_grad.reshape(length, kv_count, group_size, head_dim)
    scores = attention_probs(grouped, key_rows, allowed, head_dim)
    weights_prob = jnp.exp(scores - log_total)
    value_grad = jnp.einsum(
        "ngqk,qngd->knd", weights_prob.astype(bf16), attended_grad, preferred_element_type=f32
    )
    prob_grad = jnp.einsum("qngd,knd->ngqk", attended_grad, value_rows, preferred_element_type=f32)
    score_grad = (
        weights_prob * (prob_grad - jnp.sum(weights_prob * prob_grad, axis=-1, keepdims=True))
    ).astype(bf16)
    query_grad = jnp.einsum(
        "ngqk,knd->qngd", score_grad, key_rows, preferred_element_type=f32
    ) * head_dim ** (-0.5)
    key_grad = jnp.einsum(
        "ngqk,qngd->knd", score_grad, grouped, preferred_element_type=f32
    ) * head_dim ** (-0.5)
    query_grad = rotate(
        query_grad.reshape(length, head_count, head_dim), cosine_table, sine_table, -1.0
    )
    query_grad = query_grad.reshape(length, -1).astype(bf16)
    key_grad = rotate(key_grad, cosine_table, sine_table, -1.0).reshape(length, -1).astype(bf16)
    value_grad = value_grad.reshape(length, -1).astype(bf16)
    query_w_grad = jnp.einsum("sd,sh->dh", normed, query_grad, preferred_element_type=f32)
    key_w_grad = jnp.einsum("sd,sh->dh", normed, key_grad, preferred_element_type=f32)
    value_w_grad = jnp.einsum("sd,sh->dh", normed, value_grad, preferred_element_type=f32)
    normed_one_grad = (
        jnp.einsum("sh,dh->sd", query_grad, w_query, preferred_element_type=f32)
        + jnp.einsum("sh,dh->sd", key_grad, w_key, preferred_element_type=f32)
        + jnp.einsum("sh,dh->sd", value_grad, w_value, preferred_element_type=f32)
    )
    input_part, attn_gain_grad = norm_back(inputs, scale_one, attn_gain, normed_one_grad)
    grad_in = (mixed_grad + input_part).astype(bf16)
    small = jnp.concatenate(
        [
            attn_gain_grad.reshape(-1, 128),
            ffn_gain_grad.reshape(-1, 128),
            router_grad.reshape(-1, 128),
        ],
        axis=0,
    )
    everywhere = ("wide", "narrow")
    columns = jnp.concatenate([query_w_grad, key_w_grad, value_w_grad, out_w_grad], axis=1)
    shares = lax.psum_scatter(columns.astype(bf16), everywhere, scatter_dimension=0, tiled=True)
    columns = lax.all_gather(shares, everywhere, axis=0, tiled=True).astype(f32)
    small = lax.psum(small, everywhere)
    gain_rows = model_width // 128
    query_width, key_width = (w_query.shape[1], w_key.shape[1])
    summed = (
        small[:gain_rows].reshape(-1),
        columns[:, :query_width],
        columns[:, query_width : query_width + key_width],
        columns[:, query_width + key_width : query_width + 2 * key_width],
        columns[:, query_width + 2 * key_width :],
        small[gain_rows : 2 * gain_rows].reshape(-1),
        small[2 * gain_rows :].reshape(router.shape),
    )
    return (
        hidden_out,
        grad_in,
        summed[0],
        summed[1],
        summed[2],
        summed[3],
        summed[4],
        summed[5],
        summed[6],
        gate_w_grad,
        up_w_grad,
        down_w_grad,
    )


def solution(mesh):
    return jax.shard_map(
        on_device,
        mesh=mesh,
        in_specs=(
            P(("wide", "narrow"), None),
            P(("wide", "narrow"), None),
            P(("wide", "narrow"), None),
            P(),
            P(),
            P(),
            P(),
            P(),
            P(),
            P(),
            P("wide", None, "narrow"),
            P("wide", None, "narrow"),
            P("wide", "narrow", None),
            P(("wide", "narrow"), None),
        ),
        out_specs=(
            P(("wide", "narrow"), None),
            P(("wide", "narrow"), None),
            P(),
            P(),
            P(),
            P(),
            P(),
            P(),
            P(),
            P("wide", None, "narrow"),
            P("wide", None, "narrow"),
            P("wide", "narrow", None),
        ),
        check_vma=False,
    )
```

profile of v0, /device:TPU:0, one launch (start us, length us, event | category | flops | bytes accessed | tf_op | source)
XLA Modules:
  0.0 1261.6 jit_solution(9160530426510023094)
XLA Ops:
  8.0 1.6 fusion.15
  10.2 0.9 broadcast_multiply_fusion
  11.2 1.0 fusion.53
  12.2 2.4 convolution_convert_fusion.8
  14.6 0.9 fusion.78
  15.5 1.4 fusion.76
  17.5 7.8 fusion.83
  25.3 8.2 exponential_reduce_fusion
  33.6 8.5 fusion.25
  42.1 1.4 multiply_reduce_fusion.2
  44.8 1.2 multiply_convert_fusion.3
  48.0 1.6 fusion.69
  51.5 7.3 all-to-all-start
  58.9 116.9 %all-gather.7.cloned.1.call-done = bf16[8192,1024]{1,0:T(8,128)(2,1)} async-done(((bf16[512,1024]{1,0:T(8,128)(2,1)}), bf16[8192,1024]{1,0:T(8,128)(2,1)}) %all-gather.7.cloned.1.call-update) | async-done | bytes 16777232 | tf_op jit(solution)/shard_map/all_gather | solution.py:117
  175.9 16.5 %fusion.47 = f32[8192,512]{1,0:T(8,128)} fusion(bf16[8192,1024]{1,0:T(8,128)(2,1)} %all-gather.7.cloned.1.call-done, bf16[1,1024,512]{2,1,0:T(8,128)(2,1)} %all-gather.11.cloned.1.call-done), kind=kOutput, calls=%fused_computation.74 | convolution fusion | flops 8589934592 | bytes 34603008 | tf_op jit(solution)/shard_map/dot_general | solution.py:119
  192.4 4.5 all-gather.9.cloned.1.call-done
  196.9 16.0 %fusion.51 = f32[8192,512]{1,0:T(8,128)} fusion(bf16[8192,1024]{1,0:T(8,128)(2,1)} %all-gather.7.cloned.1.call-done, bf16[1,1024,512]{2,1,0:T(8,128)(2,1)} %all-gather.9.cloned.1.call-done), kind=kOutput, calls=%fused_computation.78 | convolution fusion | flops 8589934592 | bytes 34603008 | tf_op jit(solution)/shard_map/dot_general | solution.py:118
  212.8 6.7 all-gather.13.cloned.1.call-done
  219.6 128.5 %all-gather.15.cloned.1.call-done = bf16[8192,1024]{1,0:T(8,128)(2,1)} async-done(((bf16[512,1024]{1,0:T(8,128)(2,1)}), bf16[8192,1024]{1,0:T(8,128)(2,1)}) %all-gather.15.cloned.1.call-update) | async-done | bytes 16777232 | tf_op jit(solution)/shard_map/all_gather | solution.py:74
  348.1 32.2 %multiply_convert_fusion = (bf16[8192,512]{1,0:T(8,128)(2,1)}, bf16[8192,512]{1,0:T(8,128)(2,1)}, bf16[8192,512]{1,0:T(8,128)(2,1)}) fusion(f32[8192,512]{1,0:T(8,128)} %fusion.51, f32[8192,512]{1,0:T(8,128)} %fusion.47, bf16[1,512,1024]{2,1,0:T(8,128)(2,1)} %all-gather.13.cloned.1.call-done, bf16[8192,1024]{1,0:T(8,128)(2,1)} %all-gather.15.cloned.1.call-done, ...), kind=kOutput, calls=%fused_computation.13 | convolution fusion | flops 8682209280 | bytes 76578816 | tf_op jit(solution)/shard_map/rd,fd->rf/dot_general | solution.py:137
  380.3 18.8 %fusion.49 = f32[8192,1024]{1,0:T(8,128)} fusion(bf16[8192,512]{1,0:T(8,128)(2,1)} %get-tuple-element.65, bf16[1,1024,512]{2,1,0:T(8,128)(2,1)S(1)} %copy-done.62), kind=kOutput, calls=%fused_computation.76 | convolution fusion | flops 8589934592 | bytes 42991616 | tf_op jit(solution)/shard_map/rf,df->rd/dot_general | solution.py:147
  399.1 21.5 %add_convert_fusion = bf16[8192,1024]{1,0:T(8,128)(2,1)} fusion(f32[8192,1024]{1,0:T(8,128)} %fusion.49, bf16[8192,512]{1,0:T(8,128)(2,1)} %get-tuple-element.64, bf16[1,1024,512]{2,1,0:T(8,128)(2,1)S(1)} %copy-done.60), kind=kOutput, calls=%fused_computation.6 | convolution fusion | flops 8606711808 | bytes 59768832 | tf_op jit(solution)/shard_map/rf,df->rd/dot_general | solution.py:148
  420.7 1.1 copy-done.61
  421.9 23.7 %fusion.1 = (f32[8192]{0:T(1024)S(1)}, bf16[8192,1024]{1,0:T(8,128)(2,1)}) fusion(bf16[8192,1024]{1,0:T(8,128)(2,1)} %all-gather.15.cloned.1.call-done, f32[8192]{0:T(1024)S(1)} %bitcast.185, bf16[8192,512]{1,0:T(8,128)(2,1)} %get-tuple-element.66, bf16[1,512,1024]{2,1,0:T(8,128)(2,1)S(1)} %copy-done.61), kind=kOutput, calls=%fused_computation.4 | convolution fusion | flops 8648646656 | bytes 43057152 | tf_op jit(solution)/shard_map/dot_general | solution.py:121
  445.7 9.3 all_to_all.21
  455.1 141.1 %reduce-scatter.11.cloned.1.call-done = bf16[512,1024]{1,0:T(8,128)(2,1)} async-done(((bf16[8192,1024]{1,0:T(8,128)(2,1)}), bf16[512,1024]{1,0:T(8,128)(2,1)}) %reduce-scatter.11.cloned.1.call-update) | async-done | bytes 1048592 | tf_op jit(solution)/shard_map/reduce_scatter | solution.py:150
  596.3 3.9 multiply_reduce_fusion
  600.2 176.6 %reduce-scatter.9.cloned.1.call-done = bf16[512,1024]{1,0:T(8,128)(2,1)} async-done(((bf16[8192,1024]{1,0:T(8,128)(2,1)}), bf16[512,1024]{1,0:T(8,128)(2,1)}) %reduce-scatter.9.cloned.1.call-update) | async-done | bytes 1048592 | tf_op jit(solution)/shard_map/reduce_scatter | solution.py:122
  776.9 4.2 subtract_add_fusion
  781.1 2.6 convolution_convert_fusion.2
  783.8 2.3 convolution_convert_fusion.5
  786.0 1.5 copy.75
  787.6 1.0 copy-done.8
  788.5 9.4 fusion.41
  797.9 16.0 %fusion.3 = (f32[8,2,512]{2,1,0:T(2,128)}, f32[8,512,512,2]{2,1,3,0:T(8,128)}) fusion(f32[8,2,512,512]{2,3,1,0:T(8,128)} %get-tuple-element.93, f32[8,2,512]{2,1,0:T(2,128)S(1)} %bitcast.181, bf16[512,8,64,1]{0,2,3,1:T(8,128)(2,1)} %bitcast.165, bf16[512,8,2,64]{0,3,2,1:T(8,128)(2,1)} %bitcast.160), kind=kOutput, calls=%fused_computation.9 | convolution fusion | flops 549445632 | bytes 35192832 | tf_op jit(solution)/shard_map/qngd,knd->ngqk/dot_general | solution.py:176
  814.0 11.1 fusion.5
  825.1 6.3 fusion.37
  831.5 1.5 convolution_multiply_fusion
  836.2 1.0 copy-done.28
  837.2 1.4 convolution_convert_fusion.1
  838.8 15.2 %pad_maximum_fusion = bf16[1024,3072]{0,1:T(8,128)(2,1)} fusion(bf16[1024,1024]{0,1:T(8,128)(2,1)S(1)} %copy-done.20, bf16[1024,512]{0,1:T(8,128)(2,1)S(1)} %convolution_convert_fusion.6, bf16[1024,512]{0,1:T(8,128)(2,1)S(1)} %convolution_convert_fusion.7, bf16[1024,1024]{0,1:T(8,128)(2,1)S(1)} %convolution_convert_fusion.1), kind=kLoop, calls=%fused_computation.23 | loop fusion | flops 25165824 | bytes 12582912 | tf_op jit(solution)/shard_map/concatenate | solution.py:211
  854.0 8.7 copy.93
  862.7 15.7 %fusion.32 = bf16[1,1024,512]{2,1,0:T(8,128)(2,1)} fusion(bf16[8192,1024]{1,0:T(8,128)(2,1)} %all-gather.7.cloned.1.call-done, bf16[8192,512]{1,0:T(8,128)(2,1)} %get-tuple-element.64), kind=kOutput, calls=%fused_computation.61 | convolution fusion | flops 8590458880 | bytes 26214400 | tf_op jit(solution)/shard_map/rd,rf->df/dot_general | solution.py:145
  878.5 16.1 %fusion.31 = bf16[1,1024,512]{2,1,0:T(8,128)(2,1)} fusion(bf16[8192,1024]{1,0:T(8,128)(2,1)} %all-gather.7.cloned.1.call-done, bf16[8192,512]{1,0:T(8,128)(2,1)} %get-tuple-element.65), kind=kOutput, calls=%fused_computation.60 | convolution fusion | flops 8590458880 | bytes 26214400 | tf_op jit(solution)/shard_map/rd,rf->df/dot_general | solution.py:144
  895.0 18.9 %fusion.38 = bf16[1,512,1024]{2,1,0:T(8,128)(2,1)} fusion(bf16[8192,512]{1,0:T(8,128)(2,1)} %get-tuple-element.66, bf16[8192,1024]{1,0:T(8,128)(2,1)} %all-gather.15.cloned.1.call-done, f32[8192]{0:T(1024)S(1)} %bitcast.186), kind=kOutput, calls=%fused_computation.66 | convolution fusion | flops 8615624704 | bytes 26247168 | tf_op jit(solution)/shard_map/rf,rd->fd/dot_general | solution.py:138
  914.0 1.3 fusion.84
  915.2 1.2 reshape.200
  916.5 2.1 fusion.88
  918.6 3.4 fusion.87
  922.0 2.6 fusion.24
  925.6 51.4 %reduce-scatter.19.cloned.1.call-done = bf16[32,3072]{1,0:T(8,128)(2,1)} async-done(((bf16[1024,3072]{1,0:T(8,128)(2,1)}), bf16[32,3072]{1,0:T(8,128)(2,1)}) %reduce-scatter.19.cloned.1.call-update) | async-done | bytes 196624 | tf_op jit(solution)/shard_map/reduce_scatter | solution.py:212
  976.9 22.2 %reduce-scatter.15.cloned.1.call-done = bf16[1,1024,256]{2,1,0:T(8,128)(2,1)} async-done(((bf16[1,1024,512]{2,1,0:T(8,128)(2,1)}), bf16[1,1024,256]{2,1,0:T(8,128)(2,1)}) %reduce-scatter.15.cloned.1.call-update) | async-done | bytes 524304 | tf_op jit(solution)/shard_map/reduce_scatter | solution.py:155
  999.1 2.1 convert_element_type.169
  1001.2 21.0 %reduce-scatter.13.cloned.1.call-done = bf16[1,1024,256]{2,1,0:T(8,128)(2,1)} async-done(((bf16[1,1024,512]{2,1,0:T(8,128)(2,1)}), bf16[1,1024,256]{2,1,0:T(8,128)(2,1)}) %reduce-scatter.13.cloned.1.call-update) | async-done | bytes 524304 | tf_op jit(solution)/shard_map/reduce_scatter | solution.py:152
  1022.2 2.1 convert_element_type.166
  1024.3 21.2 %reduce-scatter.17.cloned.1.call-done = bf16[1,256,1024]{2,1,0:T(8,128)(2,1)} async-done(((bf16[1,512,1024]{2,1,0:T(8,128)(2,1)}), bf16[1,256,1024]{2,1,0:T(8,128)(2,1)}) %reduce-scatter.17.cloned.1.call-update) | async-done | bytes 524304 | tf_op jit(solution)/shard_map/reduce_scatter | solution.py:158
  1045.5 2.1 convert_element_type.172
  1047.6 3.8 fusion.21
  1051.4 120.4 %all-reduce.2.cloned.1.call-done = f32[144,128]{1,0:T(8,128)} async-done(((f32[144,128]{1,0:T(8,128)}), f32[144,128]{1,0:T(8,128)}) %all-reduce.2.cloned.1.call-update) | async-done | bytes 73744 | tf_op jit(solution)/shard_map/psum | solution.py:214
  1171.8 0.8 slice.74
  1173.6 1.3 slice_bitcast_fusion
  1174.9 71.2 %all-gather.17.cloned.1.call-done = bf16[1024,3072]{1,0:T(8,128)(2,1)} async-done(((bf16[32,3072]{1,0:T(8,128)(2,1)}), bf16[1024,3072]{1,0:T(8,128)(2,1)}) %all-gather.17.cloned.1.call-update) | async-done | bytes 6291472 | tf_op jit(solution)/shard_map/all_gather | solution.py:213
  1246.1 4.3 fusion.82
  1250.4 4.4 fusion.81
  (182 shorter events, 13.1 us)
Async XLA Ops:
  7.2 34.9 %copy-start = (bf16[1024,1024]{1,0:T(8,128)(2,1)S(1)}, bf16[1024,1024]{1,0:T(8,128)(2,1)}, u32[]{:S(2)}) copy-start(bf16[1024,1024]{1,0:T(8,128)(2,1)} %param.21) | copy-start | bytes 6291460
  7.2 7.4 copy-start.5
  7.2 7.4 copy-start.55
  7.2 51.7 %all-gather.11.cloned.1.call-start = ((), (), s32[]{:S(2)}) async-start(), calls=%async_computation.10 | async-start | bytes 1572864 | tf_op jit(solution)/shard_map/all_gather | solution.py:77
  8.0 167.9 %all-gather.7.cloned.1.call-start = ((), (), s32[]{:S(2)}) async-start(), calls=%async_computation.8 | async-start | bytes 17825792 | tf_op jit(solution)/shard_map/all_gather | solution.py:117
  8.0 6.6 copy-start.26
  9.6 5.8 copy-start.59
  10.2 6.6 copy-start.52
  11.2 5.9 copy-start.21
  14.6 19.0 %copy-start.13 = (bf16[512,512]{0,1:T(8,128)(2,1)}, bf16[512,512]{0,1:T(8,128)(2,1)S(1)}, u32[]{:S(2)}) copy-start(bf16[512,512]{0,1:T(8,128)(2,1)S(1)} %convolution_convert_fusion.8) | copy-start | bytes 1572868
  17.1 8.2 copy-start.29
  17.1 8.2 copy-start.31
  17.5 7.8 copy-start.14
  17.5 7.8 copy-start.16
  33.6 8.5 copy-start.33
  42.1 2.7 copy-start.46
  43.5 4.5 copy-start.54
  43.5 4.5 copy-start.40
  46.1 150.8 %all-gather.9.cloned.1.call-start = ((), (), s32[]{:S(2)}) async-start(), calls=%async_computation.9 | async-start | bytes 1572864 | tf_op jit(solution)/shard_map/all_gather | solution.py:76
  46.8 172.8 %all-gather.13.cloned.1.call-start = ((), (), s32[]{:S(2)}) async-start(), calls=%async_computation.11 | async-start | bytes 1572864 | tf_op jit(solution)/shard_map/all_gather | solution.py:78
  47.4 300.7 %all-gather.15.cloned.1.call-start = ((), (), s32[]{:S(2)}) async-start(), calls=%async_computation.13 | async-start | bytes 17825792 | tf_op jit(solution)/shard_map/all_gather | solution.py:74
  51.5 161.3 %all-to-all-start = ((f32[16,1,512]{2,1,0:T(1,128)}), f32[16,1,512]{2,1,0:T(1,128)S(1)}, u32[]{:S(2)}, u32[]{:S(2)}) async-start(f32[16,1,512]{2,1,0:T(1,128)} %copy.73), calls=%async_computation | async-start | bytes 65536 | tf_op jit(solution)/shard_map/all_to_all | solution.py:115
  58.9 537.4 %reduce-scatter.11.cloned.1.call-start = ((), (), s32[]{:S(2)}) async-start(), calls=%async_computation.14 | async-start | bytes 17825792 | tf_op jit(solution)/shard_map/reduce_scatter | solution.py:150
  212.8 207.9 %copy-start.50 = (f32[16,1,512]{2,1,0:T(1,128)}, f32[16,1,512]{2,1,0:T(1,128)S(1)}, u32[]{:S(2)}) copy-start(f32[16,1,512]{2,1,0:T(1,128)S(1)} %all-to-all-done) | copy-start | bytes 98308
  348.1 32.2 %copy-start.62 = (bf16[1,1024,512]{2,1,0:T(8,128)(2,1)S(1)}, bf16[1,1024,512]{2,1,0:T(8,128)(2,1)}, u32[]{:S(2)}) copy-start(bf16[1,1024,512]{2,1,0:T(8,128)(2,1)} %all-gather.9.cloned.1.call-done) | copy-start | bytes 3145732
  380.3 18.8 %copy-start.60 = (bf16[1,1024,512]{2,1,0:T(8,128)(2,1)S(1)}, bf16[1,1024,512]{2,1,0:T(8,128)(2,1)}, u32[]{:S(2)}) copy-start(bf16[1,1024,512]{2,1,0:T(8,128)(2,1)} %all-gather.11.cloned.1.call-done) | copy-start | bytes 3145732
  420.7 356.2 %reduce-scatter.9.cloned.1.call-start = ((), (), s32[]{:S(2)}) async-start(), calls=%async_computation.12 | async-start | bytes 17825792 | tf_op jit(solution)/shard_map/reduce_scatter | solution.py:122
  445.6 9.5 copy-start.24
  445.6 9.5 copy-start.39
  445.6 9.5 copy-start.43
  445.6 9.5 copy-start.45
  445.6 150.7 %copy-start.41 = (bf16[1024,16]{0,1:T(8,128)(2,1)S(1)}, bf16[1024,16]{0,1:T(8,128)(2,1)}, u32[]{:S(2)}) copy-start(bf16[1024,16]{0,1:T(8,128)(2,1)} %param.23) | copy-start | bytes 98308
  445.6 150.7 %copy-start.47 = (f32[1024]{0:T(1024)S(1)}, f32[1024]{0:T(1024)}, u32[]{:S(2)}) copy-start(f32[1024]{0:T(1024)} %param.22) | copy-start | bytes 12292
  445.6 150.7 %copy-start.49 = (f32[512]{0:T(512)S(1)}, f32[512]{0:T(512)}, u32[]{:S(2)}) copy-start(f32[512]{0:T(512)} %copy-done.48) | copy-start | bytes 6148
  445.7 331.2 %copy-start.10 = (bf16[512,1024]{1,0:T(8,128)(2,1)S(1)}, bf16[512,1024]{1,0:T(8,128)(2,1)}, u32[]{:S(2)}) copy-start(bf16[512,1024]{1,0:T(8,128)(2,1)} %param.27) | copy-start | bytes 3145732
  445.7 331.2 %copy-start.58 = (f32[512]{0:T(512)S(1)}, f32[512]{0:T(512)}, u32[]{:S(2)}) copy-start(f32[512]{0:T(512)} %get-tuple-element.87) | copy-start | bytes 6148
  445.7 531.2 %reduce-scatter.19.cloned.1.call-start = ((), (), s32[]{:S(2)}) async-start(), calls=%async_computation.20 | async-start | bytes 6488064 | tf_op jit(solution)/shard_map/reduce_scatter | solution.py:212
  455.1 326.0 %copy-start.36 = (f32[16,1,512]{2,1,0:T(1,128)}, f32[16,1,512]{2,1,0:T(1,128)S(1)}, u32[]{:S(2)}) copy-start(f32[16,1,512]{2,1,0:T(1,128)S(1)} %all_to_all.21) | copy-start | bytes 98308
  776.9 4.2 copy-start.12
  781.1 2.6 copy-start.9
  783.8 4.8 copy-start.34
  788.5 25.4 %slice-start = ((s8[16777216]{0:T(1024)(128)(4,1)}), s8[4194304]{0:T(1024)(128)(4,1)S(1)}, s32[]{:S(2)}) async-start(s8[16777216]{0:T(1024)(128)(4,1)} %bitcast.157), calls=%async_computation.21 | async-start | bytes 8388608
  788.5 25.4 %slice-start.1 = ((s8[16777216]{0:T(1024)(128)(4,1)}), s8[4194304]{0:T(1024)(128)(4,1)S(1)}, s32[]{:S(2)}) async-start(s8[16777216]{0:T(1024)(128)(4,1)} %bitcast.157), calls=%async_computation.22 | async-start | bytes 8388608
  797.9 16.0 %slice-start.2 = ((s8[16777216]{0:T(1024)(128)(4,1)}), s8[4194304]{0:T(1024)(128)(4,1)S(1)}, s32[]{:S(2)}) async-start(s8[16777216]{0:T(1024)(128)(4,1)} %bitcast.157), calls=%async_computation.23 | async-start | bytes 8388608
  797.9 16.0 %slice-start.3 = ((s8[16777216]{0:T(1024)(128)(4,1)}), s8[4194304]{0:T(1024)(128)(4,1)S(1)}, s32[]{:S(2)}) async-start(s8[16777216]{0:T(1024)(128)(4,1)} %bitcast.157), calls=%async_computation.24 | async-start | bytes 8388608
  813.9 11.1 copy-start.15
  825.1 6.3 copy-start.1
  825.1 6.3 copy-start.30
  825.1 6.3 copy-start.32
  831.5 2.4 copy-start.22
  862.7 136.5 %reduce-scatter.15.cloned.1.call-start = ((), (), s32[]{:S(2)}) async-start(), calls=%async_computation.18 | async-start | bytes 1572864 | tf_op jit(solution)/shard_map/reduce_scatter | solution.py:155
  878.5 16.5 %copy-start.51 = (f32[16,1,512]{2,1,0:T(1,128)S(1)}, f32[16,1,512]{2,1,0:T(1,128)}, u32[]{:S(2)}) copy-start(f32[16,1,512]{2,1,0:T(1,128)} %copy-done.50) | copy-start | bytes 98308
  878.5 143.7 %reduce-scatter.13.cloned.1.call-start = ((), (), s32[]{:S(2)}) async-start(), calls=%async_computation.17 | async-start | bytes 1572864 | tf_op jit(solution)/shard_map/reduce_scatter | solution.py:152
  894.7 19.2 %copy-start.4 = (bf16[512,1024]{1,0:T(8,128)(2,1)S(1)}, bf16[512,1024]{1,0:T(8,128)(2,1)}, u32[]{:S(2)}) copy-start(bf16[512,1024]{1,0:T(8,128)(2,1)} %multiply_convert_fusion.3) | copy-start | bytes 3145732
  894.7 19.2 %copy-start.25 = (f32[512,16]{0,1:T(8,128)S(1)}, f32[512,16]{0,1:T(8,128)}, u32[]{:S(2)}) copy-start(f32[512,16]{0,1:T(8,128)} %copy-done.23) | copy-start | bytes 98308
  894.7 19.2 %copy-start.37 = (f32[16,1,512]{2,1,0:T(1,128)S(1)}, f32[16,1,512]{2,1,0:T(1,128)}, u32[]{:S(2)}) copy-start(f32[16,1,512]{2,1,0:T(1,128)} %copy-done.36) | copy-start | bytes 98308
  894.7 150.8 %reduce-scatter.17.cloned.1.call-start = ((), (), s32[]{:S(2)}) async-start(), calls=%async_computation.19 | async-start | bytes 1572864 | tf_op jit(solution)/shard_map/reduce_scatter | solution.py:158
  913.9 257.9 %all-reduce.2.cloned.1.call-start = ((), (), s32[]{:S(2)}) async-start(), calls=%async_computation.15 | async-start | bytes 147456 | tf_op jit(solution)/shard_map/psum | solution.py:214
  918.6 3.4 copy-start.7
  918.6 3.4 copy-start.18
  918.6 3.4 copy-start.27
  924.6 123.0 %copy-start.57 = (f32[512]{0:T(512)S(1)}, f32[512]{0:T(512)}, u32[]{:S(2)}) copy-start(f32[512]{0:T(512)} %get-tuple-element.85) | copy-start | bytes 6148
  925.3 320.8 %all-gather.17.cloned.1.call-start = ((), (), s32[]{:S(2)}) async-start(), calls=%async_computation.16 | async-start | bytes 6488064 | tf_op jit(solution)/shard_map/all_gather | solution.py:213
  1246.1 4.3 copy-start.3
  (17 other events, 21.8 us)
Sparse Core Ops, SparseCore 0:
  9.6 23.9 all-gather.10
  46.2 129.6 all-gather.6
  177.4 19.4 all-gather.8
  198.3 21.2 all-gather.12
  221.6 126.4 all-gather.14
  420.8 175.4 reduce-scatter.10
  600.4 176.4 reduce-scatter.8
  862.8 114.0 reduce-scatter.18
  979.7 19.3 reduce-scatter.14
  1001.8 20.3 reduce-scatter.12
  1025.0 20.3 reduce-scatter.16
  1051.5 120.2 all-reduce.1
  1174.7 71.3 all-gather.16
where the time goes:
time: 1270 us; the launch traced here: 1260 us
  waiting for transfers between devices  884 us (70%)
  matrix products  258 us (20%)
  other arithmetic  56.7 us (4%)
  local copies, waits for them, and re-layouts  30 us (2%)
  between operations  15.1 us (1%)
    reduce_scatter x1, waiting for transfers between devices, on_device(): lax.psum_scatter((row_gates * outputs.astype(f32)).astype(bf16), 'wide',...  177 us
    reduce_scatter x1, waiting for transfers between devices, on_device(): lax.psum_scatter(copy_grads, 'wide', scatter_dimension=0, tiled=True)  141 us
    all_gather x1, waiting for transfers between devices, on_device(): rows_grad = lax.all_gather(grad_out, 'wide', axis=0, tiled=True)  128 us
    psum x1, waiting for transfers between devices, on_device(): small = lax.psum(small, everywhere)  120 us
    all_gather x1, waiting for transfers between devices, on_device(): rows_in = lax.all_gather(ffn_normed, 'wide', axis=0, tiled=True)  117 us
    all_gather x1, waiting for transfers between devices, on_device(): columns = lax.all_gather(shares, everywhere, axis=0, tiled=True).astype(f32)  71.2 us
    reduce_scatter x1, waiting for transfers between devices, on_device(): lax.psum_scatter(columns.astype(bf16), everywhere, scatter_dimension=0, t...  51.4 us
    dot_general x1, matrix products, on_device(): jnp.einsum('rd,fd->rf', grads_in, full_down[0], preferred_element_type=f32)  32.2 us
  transfers between devices with their start and end apart: 14, of which 12 were waited for; matrix products, arithmetic and copies ran while one was open for 14% of the time, Pallas kernels for 0%

commit v1 on v0

--- a/solution.py
+++ b/solution.py
@@ -211,7 +211,7 @@
     columns = jnp.concatenate([query_w_grad, key_w_grad, value_w_grad, out_w_grad], axis=1)
     shares = lax.psum_scatter(columns.astype(bf16), everywhere, scatter_dimension=0, tiled=True)
     columns = lax.all_gather(shares, everywhere, axis=0, tiled=True).astype(f32)
-    small = lax.psum(small, everywhere)
+    small = jnp.sum(lax.all_gather(small, everywhere), axis=0)
     gain_rows = model_width // 128
     query_width, key_width = (w_query.shape[1], w_key.shape[1])
     summed = (

time: 1270 us -> 1200 us (0.945)
  waiting for transfers between devices: 884 us -> 815 us
    psum x1 -> x0, waiting for transfers between devices: 120 us -> none  [on_device(): small = lax.psum(small, everywhere)]
    all_gather x0 -> x1, waiting for transfers between devices: none -> 54.6 us  [on_device(): small = jnp.sum(lax.all_gather(small, everywhere), axis=0)]
  transfers between devices with their start and end apart: 14 -> 14, of which waited for: 12 -> 12; matrix products, arithmetic and copies ran while one was open for 14% -> 15% of each run, Pallas kernels for 0% -> 0%
where the time goes in v1:
time: 1200 us; the launch traced here: 1190 us
  waiting for transfers between devices  815 us (68%)
  matrix products  258 us (22%)
  other arithmetic  58.5 us (5%)
  local copies, waits for them, and re-layouts  28.5 us (2%)
  between operations  15.1 us (1%)
    reduce_scatter x1, waiting for transfers between devices, on_device(): lax.psum_scatter((row_gates * outputs.astype(f32)).astype(bf16), 'wide',...  177 us
    reduce_scatter x1, waiting for transfers between devices, on_device(): lax.psum_scatter(copy_grads, 'wide', scatter_dimension=0, tiled=True)  141 us
    all_gather x1, waiting for transfers between devices, on_device(): rows_grad = lax.all_gather(grad_out, 'wide', axis=0, tiled=True)  128 us
    all_gather x1, waiting for transfers between devices, on_device(): rows_in = lax.all_gather(ffn_normed, 'wide', axis=0, tiled=True)  117 us
    all_gather x1, waiting for transfers between devices, on_device(): columns = lax.all_gather(shares, everywhere, axis=0, tiled=True).astype(f32)  67.6 us
    all_gather x1, waiting for transfers between devices, on_device(): small = jnp.sum(lax.all_gather(small, everywhere), axis=0)  54.6 us
    reduce_scatter x1, waiting for transfers between devices, on_device(): lax.psum_scatter(columns.astype(bf16), everywhere, scatter_dimension=0, t...  51.4 us
    dot_general x1, matrix products, on_device(): jnp.einsum('rd,fd->rf', grads_in, full_down[0], preferred_element_type=f32)  32.2 us
  transfers between devices with their start and end apart: 14, of which 12 were waited for; matrix products, arithmetic and copies ran while one was open for 15% of the time, Pallas kernels for 0%

profile of v1, /device:TPU:0, one launch (start us, length us, event | category | flops | bytes accessed | tf_op | source)
XLA Modules:
  0.0 1192.5 jit_solution(17818200200947158228)
XLA Ops:
  8.0 1.6 fusion.15
  10.2 0.9 broadcast_multiply_fusion
  11.2 1.0 fusion.53
  12.2 2.4 convolution_convert_fusion.8
  14.6 0.9 fusion.78
  15.5 1.4 fusion.76
  17.5 7.8 fusion.83
  25.3 8.2 exponential_reduce_fusion
  33.6 8.5 fusion.25
  42.1 1.4 multiply_reduce_fusion.2
  44.8 1.2 multiply_convert_fusion.3
  48.0 1.6 fusion.69
  51.5 7.3 all-to-all-start
  58.9 116.9 %all-gather.9.cloned.1.call-done = bf16[8192,1024]{1,0:T(8,128)(2,1)} async-done(((bf16[512,1024]{1,0:T(8,128)(2,1)}), bf16[8192,1024]{1,0:T(8,128)(2,1)}) %all-gather.9.cloned.1.call-update) | async-done | bytes 16777232 | tf_op jit(solution)/shard_map/all_gather | solution.py:117
  175.9 16.5 %fusion.47 = f32[8192,512]{1,0:T(8,128)} fusion(bf16[8192,1024]{1,0:T(8,128)(2,1)} %all-gather.9.cloned.1.call-done, bf16[1,1024,512]{2,1,0:T(8,128)(2,1)} %all-gather.13.cloned.1.call-done), kind=kOutput, calls=%fused_computation.74 | convolution fusion | flops 8589934592 | bytes 34603008 | tf_op jit(solution)/shard_map/dot_general | solution.py:119
  192.4 4.5 all-gather.11.cloned.1.call-done
  196.9 16.0 %fusion.51 = f32[8192,512]{1,0:T(8,128)} fusion(bf16[8192,1024]{1,0:T(8,128)(2,1)} %all-gather.9.cloned.1.call-done, bf16[1,1024,512]{2,1,0:T(8,128)(2,1)} %all-gather.11.cloned.1.call-done), kind=kOutput, calls=%fused_computation.78 | convolution fusion | flops 8589934592 | bytes 34603008 | tf_op jit(solution)/shard_map/dot_general | solution.py:118
  212.8 6.7 all-gather.15.cloned.1.call-done
  219.6 128.5 %all-gather.17.cloned.1.call-done = bf16[8192,1024]{1,0:T(8,128)(2,1)} async-done(((bf16[512,1024]{1,0:T(8,128)(2,1)}), bf16[8192,1024]{1,0:T(8,128)(2,1)}) %all-gather.17.cloned.1.call-update) | async-done | bytes 16777232 | tf_op jit(solution)/shard_map/all_gather | solution.py:74
  348.1 32.2 %multiply_convert_fusion = (bf16[8192,512]{1,0:T(8,128)(2,1)}, bf16[8192,512]{1,0:T(8,128)(2,1)}, bf16[8192,512]{1,0:T(8,128)(2,1)}) fusion(f32[8192,512]{1,0:T(8,128)} %fusion.51, f32[8192,512]{1,0:T(8,128)} %fusion.47, bf16[1,512,1024]{2,1,0:T(8,128)(2,1)} %all-gather.15.cloned.1.call-done, bf16[8192,1024]{1,0:T(8,128)(2,1)} %all-gather.17.cloned.1.call-done, ...), kind=kOutput, calls=%fused_computation.13 | convolution fusion | flops 8682209280 | bytes 76578816 | tf_op jit(solution)/shard_map/rd,fd->rf/dot_general | solution.py:137
  380.3 18.8 %fusion.49 = f32[8192,1024]{1,0:T(8,128)} fusion(bf16[8192,512]{1,0:T(8,128)(2,1)} %get-tuple-element.65, bf16[1,1024,512]{2,1,0:T(8,128)(2,1)S(1)} %copy-done.62), kind=kOutput, calls=%fused_computation.76 | convolution fusion | flops 8589934592 | bytes 42991616 | tf_op jit(solution)/shard_map/rf,df->rd/dot_general | solution.py:147
  399.1 21.5 %add_convert_fusion = bf16[8192,1024]{1,0:T(8,128)(2,1)} fusion(f32[8192,1024]{1,0:T(8,128)} %fusion.49, bf16[8192,512]{1,0:T(8,128)(2,1)} %get-tuple-element.64, bf16[1,1024,512]{2,1,0:T(8,128)(2,1)S(1)} %copy-done.60), kind=kOutput, calls=%fused_computation.6 | convolution fusion | flops 8606711808 | bytes 59768832 | tf_op jit(solution)/shard_map/rf,df->rd/dot_general | solution.py:148
  420.7 1.1 copy-done.61
  421.9 23.7 %fusion.1 = (f32[8192]{0:T(1024)S(1)}, bf16[8192,1024]{1,0:T(8,128)(2,1)}) fusion(bf16[8192,1024]{1,0:T(8,128)(2,1)} %all-gather.17.cloned.1.call-done, f32[8192]{0:T(1024)S(1)} %bitcast.187, bf16[8192,512]{1,0:T(8,128)(2,1)} %get-tuple-element.66, bf16[1,512,1024]{2,1,0:T(8,128)(2,1)S(1)} %copy-done.61), kind=kOutput, calls=%fused_computation.4 | convolution fusion | flops 8648646656 | bytes 43057152 | tf_op jit(solution)/shard_map/dot_general | solution.py:121
  445.7 9.3 all_to_all.21
  455.1 141.1 %reduce-scatter.11.cloned.1.call-done = bf16[512,1024]{1,0:T(8,128)(2,1)} async-done(((bf16[8192,1024]{1,0:T(8,128)(2,1)}), bf16[512,1024]{1,0:T(8,128)(2,1)}) %reduce-scatter.11.cloned.1.call-update) | async-done | bytes 1048592 | tf_op jit(solution)/shard_map/reduce_scatter | solution.py:150
  596.3 3.9 multiply_reduce_fusion
  600.2 176.6 %reduce-scatter.9.cloned.1.call-done = bf16[512,1024]{1,0:T(8,128)(2,1)} async-done(((bf16[8192,1024]{1,0:T(8,128)(2,1)}), bf16[512,1024]{1,0:T(8,128)(2,1)}) %reduce-scatter.9.cloned.1.call-update) | async-done | bytes 1048592 | tf_op jit(solution)/shard_map/reduce_scatter | solution.py:122
  776.9 4.2 subtract_add_fusion
  781.1 2.6 convolution_convert_fusion.2
  783.8 2.3 convolution_convert_fusion.5
  786.0 1.5 copy.75
  787.6 1.0 copy-done.8
  788.5 9.4 fusion.41
  797.9 16.0 %fusion.3 = (f32[8,2,512]{2,1,0:T(2,128)}, f32[8,512,512,2]{2,1,3,0:T(8,128)}) fusion(f32[8,2,512,512]{2,3,1,0:T(8,128)} %get-tuple-element.93, f32[8,2,512]{2,1,0:T(2,128)S(1)} %bitcast.183, bf16[512,8,64,1]{0,2,3,1:T(8,128)(2,1)} %bitcast.167, bf16[512,8,2,64]{0,3,2,1:T(8,128)(2,1)} %bitcast.161), kind=kOutput, calls=%fused_computation.9 | convolution fusion | flops 549445632 | bytes 35192832 | tf_op jit(solution)/shard_map/qngd,knd->ngqk/dot_general | solution.py:176
  814.0 11.1 fusion.5
  825.1 6.3 fusion.37
  831.5 1.5 convolution_multiply_fusion
  835.3 0.8 convolution_convert_fusion.7
  836.2 1.0 copy-done.28
  837.2 1.4 convolution_convert_fusion.1
  838.8 15.2 %pad_maximum_fusion = bf16[1024,3072]{0,1:T(8,128)(2,1)} fusion(bf16[1024,1024]{0,1:T(8,128)(2,1)S(1)} %copy-done.20, bf16[1024,512]{0,1:T(8,128)(2,1)S(1)} %convolution_convert_fusion.6, bf16[1024,512]{0,1:T(8,128)(2,1)S(1)} %convolution_convert_fusion.7, bf16[1024,1024]{0,1:T(8,128)(2,1)S(1)} %convolution_convert_fusion.1), kind=kLoop, calls=%fused_computation.23 | loop fusion | flops 25165824 | bytes 12582912 | tf_op jit(solution)/shard_map/concatenate | solution.py:211
  854.0 8.7 copy.93
  862.7 15.7 %fusion.32 = bf16[1,1024,512]{2,1,0:T(8,128)(2,1)} fusion(bf16[8192,1024]{1,0:T(8,128)(2,1)} %all-gather.9.cloned.1.call-done, bf16[8192,512]{1,0:T(8,128)(2,1)} %get-tuple-element.64), kind=kOutput, calls=%fused_computation.61 | convolution fusion | flops 8590458880 | bytes 26214400 | tf_op jit(solution)/shard_map/rd,rf->df/dot_general | solution.py:145
  878.5 16.1 %fusion.31 = bf16[1,1024,512]{2,1,0:T(8,128)(2,1)} fusion(bf16[8192,1024]{1,0:T(8,128)(2,1)} %all-gather.9.cloned.1.call-done, bf16[8192,512]{1,0:T(8,128)(2,1)} %get-tuple-element.65), kind=kOutput, calls=%fused_computation.60 | convolution fusion | flops 8590458880 | bytes 26214400 | tf_op jit(solution)/shard_map/rd,rf->df/dot_general | solution.py:144
  895.0 18.9 %fusion.38 = bf16[1,512,1024]{2,1,0:T(8,128)(2,1)} fusion(bf16[8192,512]{1,0:T(8,128)(2,1)} %get-tuple-element.66, bf16[8192,1024]{1,0:T(8,128)(2,1)} %all-gather.17.cloned.1.call-done, f32[8192]{0:T(1024)S(1)} %bitcast.188), kind=kOutput, calls=%fused_computation.66 | convolution fusion | flops 8615624704 | bytes 26247168 | tf_op jit(solution)/shard_map/rf,rd->fd/dot_general | solution.py:138
  914.0 1.3 fusion.84
  915.2 1.2 reshape.200
  916.5 2.1 fusion.88
  918.6 3.4 fusion.87
  922.0 2.6 fusion.24
  925.6 51.4 %reduce-scatter.19.cloned.1.call-done = bf16[32,3072]{1,0:T(8,128)(2,1)} async-done(((bf16[1024,3072]{1,0:T(8,128)(2,1)}), bf16[32,3072]{1,0:T(8,128)(2,1)}) %reduce-scatter.19.cloned.1.call-update) | async-done | bytes 196624 | tf_op jit(solution)/shard_map/reduce_scatter | solution.py:212
  976.9 22.2 %reduce-scatter.15.cloned.1.call-done = bf16[1,1024,256]{2,1,0:T(8,128)(2,1)} async-done(((bf16[1,1024,512]{2,1,0:T(8,128)(2,1)}), bf16[1,1024,256]{2,1,0:T(8,128)(2,1)}) %reduce-scatter.15.cloned.1.call-update) | async-done | bytes 524304 | tf_op jit(solution)/shard_map/reduce_scatter | solution.py:155
  999.1 2.1 convert_element_type.169
  1001.2 21.0 %reduce-scatter.13.cloned.1.call-done = bf16[1,1024,256]{2,1,0:T(8,128)(2,1)} async-done(((bf16[1,1024,512]{2,1,0:T(8,128)(2,1)}), bf16[1,1024,256]{2,1,0:T(8,128)(2,1)}) %reduce-scatter.13.cloned.1.call-update) | async-done | bytes 524304 | tf_op jit(solution)/shard_map/reduce_scatter | solution.py:152
  1022.2 2.1 convert_element_type.166
  1024.3 21.2 %reduce-scatter.17.cloned.1.call-done = bf16[1,256,1024]{2,1,0:T(8,128)(2,1)} async-done(((bf16[1,512,1024]{2,1,0:T(8,128)(2,1)}), bf16[1,256,1024]{2,1,0:T(8,128)(2,1)}) %reduce-scatter.17.cloned.1.call-update) | async-done | bytes 524304 | tf_op jit(solution)/shard_map/reduce_scatter | solution.py:158
  1045.5 2.1 convert_element_type.172
  1047.6 3.8 fusion.21
  1051.4 54.6 %all-gather.21.cloned.1.call-done = f32[4608,128]{1,0:T(8,128)} async-done(((f32[144,128]{1,0:T(8,128)}), f32[4608,128]{1,0:T(8,128)}) %all-gather.21.cloned.1.call-update) | async-done | bytes 2359312 | tf_op jit(solution)/shard_map/all_gather | solution.py:214
  1106.0 1.8 reduce_sum.119
  1109.3 67.6 %all-gather.19.cloned.1.call-done = bf16[1024,3072]{1,0:T(8,128)(2,1)} async-done(((bf16[32,3072]{1,0:T(8,128)(2,1)}), bf16[1024,3072]{1,0:T(8,128)(2,1)}) %all-gather.19.cloned.1.call-update) | async-done | bytes 6291472 | tf_op jit(solution)/shard_map/all_gather | solution.py:213
  1177.0 4.3 fusion.82
  1181.3 4.4 fusion.81
  (183 shorter events, 12.9 us)
Async XLA Ops:
  7.2 34.9 %copy-start = (bf16[1024,1024]{1,0:T(8,128)(2,1)S(1)}, bf16[1024,1024]{1,0:T(8,128)(2,1)}, u32[]{:S(2)}) copy-start(bf16[1024,1024]{1,0:T(8,128)(2,1)} %param.21) | copy-start | bytes 6291460
  7.2 7.4 copy-start.5
  7.2 7.4 copy-start.55
  7.2 51.7 %all-gather.13.cloned.1.call-start = ((), (), s32[]{:S(2)}) async-start(), calls=%async_computation.10 | async-start | bytes 1572864 | tf_op jit(solution)/shard_map/all_gather | solution.py:77
  8.0 167.9 %all-gather.9.cloned.1.call-start = ((), (), s32[]{:S(2)}) async-start(), calls=%async_computation.8 | async-start | bytes 17825792 | tf_op jit(solution)/shard_map/all_gather | solution.py:117
  8.0 6.6 copy-start.26
  9.6 5.8 copy-start.59
  10.2 6.6 copy-start.52
  11.2 5.9 copy-start.21
  14.6 19.0 %copy-start.13 = (bf16[512,512]{0,1:T(8,128)(2,1)}, bf16[512,512]{0,1:T(8,128)(2,1)S(1)}, u32[]{:S(2)}) copy-start(bf16[512,512]{0,1:T(8,128)(2,1)S(1)} %convolution_convert_fusion.8) | copy-start | bytes 1572868
  17.1 8.2 copy-start.29
  17.1 8.2 copy-start.31
  17.5 7.8 copy-start.14
  17.5 7.8 copy-start.16
  33.6 8.5 copy-start.33
  42.1 2.7 copy-start.46
  43.5 4.5 copy-start.54
  43.5 4.5 copy-start.40
  46.1 150.8 %all-gather.11.cloned.1.call-start = ((), (), s32[]{:S(2)}) async-start(), calls=%async_computation.9 | async-start | bytes 1572864 | tf_op jit(solution)/shard_map/all_gather | solution.py:76
  46.8 172.8 %all-gather.15.cloned.1.call-start = ((), (), s32[]{:S(2)}) async-start(), calls=%async_computation.11 | async-start | bytes 1572864 | tf_op jit(solution)/shard_map/all_gather | solution.py:78
  47.4 300.7 %all-gather.17.cloned.1.call-start = ((), (), s32[]{:S(2)}) async-start(), calls=%async_computation.13 | async-start | bytes 17825792 | tf_op jit(solution)/shard_map/all_gather | solution.py:74
  51.5 161.3 %all-to-all-start = ((f32[16,1,512]{2,1,0:T(1,128)}), f32[16,1,512]{2,1,0:T(1,128)S(1)}, u32[]{:S(2)}, u32[]{:S(2)}) async-start(f32[16,1,512]{2,1,0:T(1,128)} %copy.73), calls=%async_computation | async-start | bytes 65536 | tf_op jit(solution)/shard_map/all_to_all | solution.py:115
  58.9 537.4 %reduce-scatter.11.cloned.1.call-start = ((), (), s32[]{:S(2)}) async-start(), calls=%async_computation.14 | async-start | bytes 17825792 | tf_op jit(solution)/shard_map/reduce_scatter | solution.py:150
  212.8 207.9 %copy-start.50 = (f32[16,1,512]{2,1,0:T(1,128)}, f32[16,1,512]{2,1,0:T(1,128)S(1)}, u32[]{:S(2)}) copy-start(f32[16,1,512]{2,1,0:T(1,128)S(1)} %all-to-all-done) | copy-start | bytes 98308
  348.1 32.2 %copy-start.62 = (bf16[1,1024,512]{2,1,0:T(8,128)(2,1)S(1)}, bf16[1,1024,512]{2,1,0:T(8,128)(2,1)}, u32[]{:S(2)}) copy-start(bf16[1,1024,512]{2,1,0:T(8,128)(2,1)} %all-gather.11.cloned.1.call-done) | copy-start | bytes 3145732
  380.3 18.8 %copy-start.60 = (bf16[1,1024,512]{2,1,0:T(8,128)(2,1)S(1)}, bf16[1,1024,512]{2,1,0:T(8,128)(2,1)}, u32[]{:S(2)}) copy-start(bf16[1,1024,512]{2,1,0:T(8,128)(2,1)} %all-gather.13.cloned.1.call-done) | copy-start | bytes 3145732
  420.7 356.2 %reduce-scatter.9.cloned.1.call-start = ((), (), s32[]{:S(2)}) async-start(), calls=%async_computation.12 | async-start | bytes 17825792 | tf_op jit(solution)/shard_map/reduce_scatter | solution.py:122
  445.6 9.5 copy-start.24
  445.6 9.5 copy-start.39
  445.6 9.5 copy-start.43
  445.6 9.5 copy-start.45
  445.6 150.7 %copy-start.41 = (bf16[1024,16]{0,1:T(8,128)(2,1)S(1)}, bf16[1024,16]{0,1:T(8,128)(2,1)}, u32[]{:S(2)}) copy-start(bf16[1024,16]{0,1:T(8,128)(2,1)} %param.23) | copy-start | bytes 98308
  445.6 150.7 %copy-start.47 = (f32[1024]{0:T(1024)S(1)}, f32[1024]{0:T(1024)}, u32[]{:S(2)}) copy-start(f32[1024]{0:T(1024)} %param.22) | copy-start | bytes 12292
  445.6 150.7 %copy-start.49 = (f32[512]{0:T(512)S(1)}, f32[512]{0:T(512)}, u32[]{:S(2)}) copy-start(f32[512]{0:T(512)} %copy-done.48) | copy-start | bytes 6148
  445.7 331.2 %copy-start.10 = (bf16[512,1024]{1,0:T(8,128)(2,1)S(1)}, bf16[512,1024]{1,0:T(8,128)(2,1)}, u32[]{:S(2)}) copy-start(bf16[512,1024]{1,0:T(8,128)(2,1)} %param.27) | copy-start | bytes 3145732
  445.7 331.2 %copy-start.58 = (f32[512]{0:T(512)S(1)}, f32[512]{0:T(512)}, u32[]{:S(2)}) copy-start(f32[512]{0:T(512)} %get-tuple-element.87) | copy-start | bytes 6148
  445.7 531.2 %reduce-scatter.19.cloned.1.call-start = ((), (), s32[]{:S(2)}) async-start(), calls=%async_computation.20 | async-start | bytes 6488064 | tf_op jit(solution)/shard_map/reduce_scatter | solution.py:212
  455.1 326.0 %copy-start.36 = (f32[16,1,512]{2,1,0:T(1,128)}, f32[16,1,512]{2,1,0:T(1,128)S(1)}, u32[]{:S(2)}) copy-start(f32[16,1,512]{2,1,0:T(1,128)S(1)} %all_to_all.21) | copy-start | bytes 98308
  776.9 4.2 copy-start.12
  781.1 2.6 copy-start.9
  783.8 4.8 copy-start.34
  788.5 25.4 %slice-start = ((s8[16777216]{0:T(1024)(128)(4,1)}), s8[4194304]{0:T(1024)(128)(4,1)S(1)}, s32[]{:S(2)}) async-start(s8[16777216]{0:T(1024)(128)(4,1)} %bitcast.158), calls=%async_computation.21 | async-start | bytes 8388608
  788.5 25.4 %slice-start.1 = ((s8[16777216]{0:T(1024)(128)(4,1)}), s8[4194304]{0:T(1024)(128)(4,1)S(1)}, s32[]{:S(2)}) async-start(s8[16777216]{0:T(1024)(128)(4,1)} %bitcast.158), calls=%async_computation.22 | async-start | bytes 8388608
  797.9 16.0 %slice-start.2 = ((s8[16777216]{0:T(1024)(128)(4,1)}), s8[4194304]{0:T(1024)(128)(4,1)S(1)}, s32[]{:S(2)}) async-start(s8[16777216]{0:T(1024)(128)(4,1)} %bitcast.158), calls=%async_computation.23 | async-start | bytes 8388608
  797.9 16.0 %slice-start.3 = ((s8[16777216]{0:T(1024)(128)(4,1)}), s8[4194304]{0:T(1024)(128)(4,1)S(1)}, s32[]{:S(2)}) async-start(s8[16777216]{0:T(1024)(128)(4,1)} %bitcast.158), calls=%async_computation.24 | async-start | bytes 8388608
  813.9 11.1 copy-start.15
  825.1 6.3 copy-start.1
  825.1 6.3 copy-start.30
  825.1 6.3 copy-start.32
  831.5 2.4 copy-start.22
  862.7 136.5 %reduce-scatter.15.cloned.1.call-start = ((), (), s32[]{:S(2)}) async-start(), calls=%async_computation.17 | async-start | bytes 1572864 | tf_op jit(solution)/shard_map/reduce_scatter | solution.py:155
  878.5 16.5 %copy-start.51 = (f32[16,1,512]{2,1,0:T(1,128)S(1)}, f32[16,1,512]{2,1,0:T(1,128)}, u32[]{:S(2)}) copy-start(f32[16,1,512]{2,1,0:T(1,128)} %copy-done.50) | copy-start | bytes 98308
  878.5 143.7 %reduce-scatter.13.cloned.1.call-start = ((), (), s32[]{:S(2)}) async-start(), calls=%async_computation.16 | async-start | bytes 1572864 | tf_op jit(solution)/shard_map/reduce_scatter | solution.py:152
  894.7 19.2 %copy-start.4 = (bf16[512,1024]{1,0:T(8,128)(2,1)S(1)}, bf16[512,1024]{1,0:T(8,128)(2,1)}, u32[]{:S(2)}) copy-start(bf16[512,1024]{1,0:T(8,128)(2,1)} %multiply_convert_fusion.3) | copy-start | bytes 3145732
  894.7 19.2 %copy-start.25 = (f32[512,16]{0,1:T(8,128)S(1)}, f32[512,16]{0,1:T(8,128)}, u32[]{:S(2)}) copy-start(f32[512,16]{0,1:T(8,128)} %copy-done.23) | copy-start | bytes 98308
  894.7 19.2 %copy-start.37 = (f32[16,1,512]{2,1,0:T(1,128)S(1)}, f32[16,1,512]{2,1,0:T(1,128)}, u32[]{:S(2)}) copy-start(f32[16,1,512]{2,1,0:T(1,128)} %copy-done.36) | copy-start | bytes 98308
  894.7 150.8 %reduce-scatter.17.cloned.1.call-start = ((), (), s32[]{:S(2)}) async-start(), calls=%async_computation.18 | async-start | bytes 1572864 | tf_op jit(solution)/shard_map/reduce_scatter | solution.py:158
  913.9 192.1 %all-gather.21.cloned.1.call-start = ((), (), s32[]{:S(2)}) async-start(), calls=%async_computation.19 | async-start | bytes 2433024 | tf_op jit(solution)/shard_map/all_gather | solution.py:214
  918.6 3.4 copy-start.7
  918.6 3.4 copy-start.18
  918.6 3.4 copy-start.27
  924.6 123.0 %copy-start.57 = (f32[512]{0:T(512)S(1)}, f32[512]{0:T(512)}, u32[]{:S(2)}) copy-start(f32[512]{0:T(512)} %get-tuple-element.85) | copy-start | bytes 6148
  925.3 251.7 %all-gather.19.cloned.1.call-start = ((), (), s32[]{:S(2)}) async-start(), calls=%async_computation.15 | async-start | bytes 6488064 | tf_op jit(solution)/shard_map/all_gather | solution.py:213
  1177.0 4.3 copy-start.3
  (17 other events, 21.8 us)
Sparse Core Ops, SparseCore 0:
  9.6 23.9 all-gather.12
  46.2 129.6 all-gather.8
  177.4 19.4 all-gather.10
  198.3 21.2 all-gather.14
  221.6 126.4 all-gather.16
  420.8 175.4 reduce-scatter.10
  600.4 176.4 reduce-scatter.8
  862.8 114.0 reduce-scatter.18
  979.7 19.3 reduce-scatter.14
  1001.8 20.3 reduce-scatter.12
  1025.0 20.3 reduce-scatter.16
  1048.8 57.0 all-gather.20
  1108.8 68.0 all-gather.18
